TPU v7x, 32 devices: a whole 2x2x4 slice. The times are simulated.
32 devices in a mesh: fsdp: 4 (over y, x), tp: 8 (over z, core).
Axes of the slice: x: 2, y: 2, z: 4, core: 2. Of those that a mesh axis runs over, the one named last changes fastest.
Arguments:
- ref_gate: bfloat16 [3072, 11008], P('fsdp', 'tp'), may hold values from -6 to 6
- ref_up: bfloat16 [3072, 11008], P('fsdp', 'tp'), may hold values from -6 to 6
- ref_residual: bfloat16 [3072, 4096], P('fsdp', 'tp'), may hold values from -6 to 6
- ref_modality: int32 [3072], P('fsdp'), may hold values 0 or 1
- ref_down_text: bfloat16 [4096, 11008], P('fsdp', 'tp'), may hold values from -0.0546875 to 0.0546875
- ref_down_image: bfloat16 [4096, 11008], P('fsdp', 'tp'), may hold values from -0.0546875 to 0.0546875
- pol_gate: bfloat16 [3072, 11008], P('fsdp', 'tp'), may hold values from -6 to 6
- pol_up: bfloat16 [3072, 11008], P('fsdp', 'tp'), may hold values from -6 to 6
- pol_modality: int32 [3072], P('fsdp'), may hold values 0 or 1
- pol_segment: int32 [3072], P('fsdp'), may hold values from 0 to 5, never falling along the last dimension, each value on 1 to 768 neighbouring positions
- pair_margin: float32 [3], replicated, may hold values from -30 to 30
- token_cotangent: bfloat16 [3072, 4096], P('fsdp', 'tp'), may hold values from -24 to 24
- pol_down_text: bfloat16 [4096, 11008], P('fsdp', 'tp'), may hold values from -0.0546875 to 0.0546875
- pol_down_image: bfloat16 [4096, 11008], P('fsdp', 'tp'), may hold values from -0.0546875 to 0.0546875
Outputs:
- ref_out: bfloat16 [3072, 4096], P('fsdp', 'tp')
- grad_gate: bfloat16 [3072, 11008], P('fsdp', 'tp')
- grad_up: bfloat16 [3072, 11008], P('fsdp', 'tp')
- grad_down_text: float32 [4096, 11008], P('fsdp', 'tp')
- grad_down_image: float32 [4096, 11008], P('fsdp', 'tp')
Inputs may be any that keep to these rules, and one draw needn't show every extreme that they name: `ref_modality`: 0 marks a text token, 1 an image token. `pol_modality`: 0 marks a text token, 1 an image token. `pol_segment`: response numbers never fall along the tokens; responses 2p and 2p + 1 are the chosen and the rejected response of pair p; every response has at least one token.
All inputs are finite; a program needn't handle non-finite values. No bound on the sum of `ref_modality` or of `pol_modality` on one device may be relied on, other than what follows from the above.
Results may differ from a plain program's by a relative error of at most 0.015.
Values may be sent and summed in bfloat16 or wider, within the bound.
A program may use at most 192 MiB of HBM per device.

v0:
```python
import jax
import jax.numpy as jnp
from jax import lax
from jax.sharding import PartitionSpec as P

dpo_beta = 0.1


def split_hidden(gate, up, modality):
    gate_f = gate.astype(jnp.float32)
    up_f = up.astype(jnp.float32)
    sig = jax.nn.sigmoid(gate_f)
    act = gate_f * sig
    hidden = (act * up_f).astype(jnp.bfloat16)
    image = (modality == 1)[:, None]
    zero = jnp.zeros_like(hidden)
    return (jnp.where(image, zero, hidden), jnp.where(image, hidden, zero), gate_f, up_f, sig, act)


def forward_term(left_text, left_image, right_text, right_image):
    contract = (((1,), (1,)), ((), ()))
    part = lax.dot_general(left_text, right_text, contract, preferred_element_type=jnp.float32)
    return part + lax.dot_general(
        left_image, right_image, contract, preferred_element_type=jnp.float32
    )


def backward_term(left_text, left_image, right_text, right_image):
    part = jnp.dot(left_text, right_text, preferred_element_type=jnp.float32)
    return part + jnp.dot(left_image, right_image, preferred_element_type=jnp.float32)


def per_device(
    ref_gate,
    ref_up,
    ref_residual,
    ref_modality,
    ref_down_text,
    ref_down_image,
    pol_gate,
    pol_up,
    pol_modality,
    pol_segment,
    pair_margin,
    token_cotangent,
    pol_down_text,
    pol_down_image,
):
    ref_text, ref_image, _, _, _, _ = split_hidden(ref_gate, ref_up, ref_modality)
    pol_text, pol_image, gate_f, up_f, sig, act = split_hidden(pol_gate, pol_up, pol_modality)
    seg_ids = jnp.arange(2 * pair_margin.shape[0], dtype=jnp.int32)
    pair_weight = dpo_beta * jax.nn.sigmoid(-dpo_beta * pair_margin)
    table = jnp.repeat(pair_weight, 2) * jnp.where(seg_ids % 2 == 0, -1.0, 1.0).astype(jnp.float32)
    coef = jnp.sum(
        jnp.where(pol_segment[:, None] == seg_ids[None, :], table[None, :], jnp.float32(0.0)),
        axis=1,
    )
    local_cot = (coef[:, None] * token_cotangent.astype(jnp.float32)).astype(jnp.bfloat16)
    full_cot = lax.all_gather(local_cot, "tp", axis=1, tiled=True)
    image_p = (pol_modality == 1)[:, None]
    zero_cot = jnp.zeros_like(full_cot)
    cot_text = jnp.where(image_p, zero_cot, full_cot)
    cot_image = jnp.where(image_p, full_cot, zero_cot)
    stacked_ref = jnp.stack([ref_down_text, ref_down_image])
    piece = lax.all_gather(stacked_ref, "fsdp", axis=1, tiled=True)
    terms = forward_term(ref_text, ref_image, piece[0], piece[1])
    d_hidden = backward_term(
        cot_text,
        cot_image,
        lax.all_gather(pol_down_text, "fsdp", axis=0, tiled=True),
        lax.all_gather(pol_down_image, "fsdp", axis=0, tiled=True),
    )
    summed = lax.psum_scatter(
        terms.astype(jnp.bfloat16), "tp", scatter_dimension=1, tiled=True
    ).astype(jnp.float32)
    ref_out = (summed + ref_residual.astype(jnp.float32)).astype(jnp.bfloat16)
    grad_gate = (d_hidden * up_f * sig * (1.0 + gate_f * (1.0 - sig))).astype(jnp.bfloat16)
    grad_up = (d_hidden * act).astype(jnp.bfloat16)
    width = pol_down_text.shape[1]
    over_rows = (((0,), (0,)), ((), ()))
    term_text = lax.dot_general(cot_text, pol_text, over_rows, preferred_element_type=jnp.float32)
    term_image = lax.dot_general(
        cot_image, pol_image, over_rows, preferred_element_type=jnp.float32
    )
    grads = lax.psum_scatter(
        jnp.concatenate([term_text, term_image], axis=1).astype(jnp.bfloat16),
        "fsdp",
        scatter_dimension=0,
        tiled=True,
    ).astype(jnp.float32)
    return (ref_out, grad_gate, grad_up, grads[:, :width], grads[:, width:])


def solution(mesh):
    in_specs = (
        P("fsdp", "tp"),
        P("fsdp", "tp"),
        P("fsdp", "tp"),
        P("fsdp"),
        P("fsdp", "tp"),
        P("fsdp", "tp"),
        P("fsdp", "tp"),
        P("fsdp", "tp"),
        P("fsdp"),
        P("fsdp"),
        P(),
        P("fsdp", "tp"),
        P("fsdp", "tp"),
        P("fsdp", "tp"),
    )
    out_specs = (
        P("fsdp", "tp"),
        P("fsdp", "tp"),
        P("fsdp", "tp"),
        P("fsdp", "tp"),
        P("fsdp", "tp"),
    )
    return jax.shard_map(
        per_device, mesh=mesh, in_specs=in_specs, out_specs=out_specs, check_vma=False
    )
```

profile of v0, /device:TPU:0, one launch (start us, length us, event | category | flops | bytes accessed | tf_op | source)
XLA Modules:
  0.0 803.0 jit_solution(6594723527638454698)
XLA Ops:
  7.2 0.0 all-gather.5.cloned.1.call-start
  7.2 5.7 pad_maximum_fusion.1
  12.9 0.0 copy-start.10
  12.9 0.0 copy-start.4
  12.9 0.0 copy-start
  12.9 0.0 all-gather.5.cloned.1.call-update
  12.9 0.0 copy-start.2
  12.9 0.0 copy-start.6
  12.9 0.0 all-gather.7.cloned.1.call-start
  13.0 0.6 copy-done.10
  13.5 0.1 broadcast_in_dim.66
  13.6 0.1 reshape.33
  13.7 0.0 copy-done.4
  13.7 0.1 select_reduce_fusion
  13.8 0.2 copy-done
  14.0 1.1 multiply_convert_fusion.1
  15.1 0.0 all-gather.7.cloned.1.call-update
  15.2 0.0 all-gather.9.cloned.1.call-start
  15.2 0.7 all-gather.9.cloned.1.call-update
  15.9 0.0 all-gather.11.cloned.1.call-start
  15.9 0.5 all-gather.11.cloned.1.call-update
  16.5 0.0 reduce-scatter.3.cloned.1.call-start
  16.5 0.0 copy-done.2
  16.5 205.2 %all-gather.5.cloned.1.call-done = bf16[2,4096,1376]{1,2,0:T(8,128)(2,1)} async-done(((bf16[2,1024,1376]{1,2,0:T(8,128)(2,1)}), bf16[2,4096,1376]{1,2,0:T(8,128)(2,1)}) %all-gather.5.cloned.1.call-update) | async-done | bytes 22544400 | tf_op jit(solution)/shard_map/all_gather | solution.py:65
  221.8 0.0 copy-done.6
  221.8 18.6 %fusion = f32[768,4096]{1,0:T(8,128)} fusion(bf16[2,4096,1376]{1,2,0:T(8,128)(2,1)} %all-gather.5.cloned.1.call-done, pred[768]{0:T(1024)(128)(4,1)S(1)} %broadcast_compare_fusion.1, bf16[768,1376]{0,1:T(8,128)(2,1)S(1)} %copy-done.6, bf16[768,1376]{0,1:T(8,128)(2,1)} %param.14), kind=kOutput, calls=%fused_computation.5 | convolution fusion | flops 8666554368 | bytes 28082944 | tf_op jit(solution)/shard_map/dot_general | solution.py:23
  240.3 0.0 copy-done.7
  240.3 18.3 %add_convert_fusion = bf16[768,4096]{1,0:T(8,128)(2,1)} fusion(f32[768,4096]{1,0:T(8,128)} %fusion, bf16[2,4096,1376]{1,2,0:T(8,128)(2,1)} %all-gather.5.cloned.1.call-done, pred[768]{0:T(1024)(128)(4,1)S(1)} %broadcast_compare_fusion.1, bf16[768,1376]{0,1:T(8,128)(2,1)S(1)} %copy-done.6, bf16[768,1376]{0,1:T(8,128)(2,1)S(1)} %copy-done.7), kind=kOutput, calls=%fused_computation.3 | convolution fusion | flops 8672845824 | bytes 34374400 | tf_op jit(solution)/shard_map/dot_general | solution.py:22
  258.7 0.0 reduce-scatter.3.cloned.1.call-update
  258.7 0.2 reduce-scatter.5.cloned.1.call-start
  258.9 0.4 copy-done.3
  259.4 29.3 %all-gather.7.cloned.1.call-done = bf16[768,4096]{1,0:T(8,128)(2,1)} async-done(((bf16[768,512]{1,0:T(8,128)(2,1)}), bf16[768,4096]{1,0:T(8,128)(2,1)}) %all-gather.7.cloned.1.call-update) | async-done | bytes 6291472 | tf_op jit(solution)/shard_map/all_gather | solution.py:59
  288.7 0.0 copy-done.8
  288.7 15.3 %convolution_convert_fusion = bf16[4096,1376]{0,1:T(8,128)(2,1)} fusion(bf16[768,4096]{1,0:T(8,128)(2,1)} %all-gather.7.cloned.1.call-done, pred[768]{0:T(1024)(128)(4,1)S(1)} %broadcast_compare_fusion, bf16[768,1376]{0,1:T(8,128)(2,1)} %param.21, bf16[768,1376]{0,1:T(8,128)(2,1)S(1)} %copy-done.8), kind=kOutput, calls=%fused_computation.1 | convolution fusion | flops 8675336192 | bytes 21791488 | tf_op jit(solution)/shard_map/dot_general | solution.py:82
  304.0 0.0 copy-done.5
  304.0 0.0 copy-done.9
  304.0 12.3 %convolution_convert_fusion.1 = bf16[4096,1376]{0,1:T(8,128)(2,1)} fusion(bf16[768,4096]{1,0:T(8,128)(2,1)S(1)} %copy-done.5, pred[768]{0:T(1024)(128)(4,1)S(1)} %broadcast_compare_fusion, bf16[768,1376]{0,1:T(8,128)(2,1)S(1)} %copy-done.9, bf16[768,1376]{0,1:T(8,128)(2,1)S(1)} %copy-done.8), kind=kOutput, calls=%fused_computation.2 | convolution fusion | flops 8675336192 | bytes 21791488 | tf_op jit(solution)/shard_map/dot_general | solution.py:81
  316.3 20.2 %pad_maximum_fusion = bf16[4096,2752]{0,1:T(8,128)(2,1)} fusion(bf16[4096,1376]{0,1:T(8,128)(2,1)} %convolution_convert_fusion, bf16[4096,1376]{0,1:T(8,128)(2,1)} %convolution_convert_fusion.1), kind=kLoop, calls=%fused_computation | loop fusion | flops 45088768 | bytes 45088768 | tf_op jit(solution)/shard_map/concatenate | solution.py:86
  336.4 0.0 reduce-scatter.5.cloned.1.call-update
  336.4 64.2 %all-gather.9.cloned.1.call-done = bf16[4096,1376]{0,1:T(8,128)(2,1)} async-done(((bf16[1024,1376]{0,1:T(8,128)(2,1)}), bf16[4096,1376]{0,1:T(8,128)(2,1)}) %all-gather.9.cloned.1.call-update) | async-done | bytes 11272208 | tf_op jit(solution)/shard_map/all_gather | solution.py:70
  400.7 15.1 %fusion.15 = f32[768,1376]{0,1:T(8,128)} fusion(bf16[4096,1376]{0,1:T(8,128)(2,1)} %all-gather.9.cloned.1.call-done, bf16[768,4096]{1,0:T(8,128)(2,1)} %all-gather.7.cloned.1.call-done, pred[768]{0:T(1024)(128)(4,1)S(1)} %broadcast_compare_fusion), kind=kOutput, calls=%fused_computation.33 | convolution fusion | flops 8660189184 | bytes 21791488 | tf_op jit(solution)/shard_map/dot_general | solution.py:29
  415.8 98.1 %all-gather.11.cloned.1.call-done = bf16[4096,1376]{0,1:T(8,128)(2,1)} async-done(((bf16[1024,1376]{0,1:T(8,128)(2,1)}), bf16[4096,1376]{0,1:T(8,128)(2,1)}) %all-gather.11.cloned.1.call-update) | async-done | bytes 11272208 | tf_op jit(solution)/shard_map/all_gather | solution.py:71
  513.9 17.5 %multiply_convert_fusion = (bf16[768,1376]{0,1:T(8,128)(2,1)}, bf16[768,1376]{0,1:T(8,128)(2,1)}) fusion(bf16[768,1376]{0,1:T(8,128)(2,1)S(1)} %copy-done.8, bf16[768,1376]{0,1:T(8,128)(2,1)} %param.21, f32[768,1376]{0,1:T(8,128)} %fusion.15, bf16[4096,1376]{0,1:T(8,128)(2,1)} %all-gather.11.cloned.1.call-done, ...), kind=kOutput, calls=%fused_computation.30 | convolution fusion | flops 8677097472 | bytes 30245632 | tf_op jit(solution)/shard_map/dot_general | solution.py:30
  531.4 54.4 %reduce-scatter.3.cloned.1.call-done = bf16[768,512]{1,0:T(8,128)(2,1)} async-done(((bf16[768,4096]{1,0:T(8,128)(2,1)}), bf16[768,512]{1,0:T(8,128)(2,1)}) %reduce-scatter.3.cloned.1.call-update) | async-done | bytes 786448 | tf_op jit(solution)/shard_map/reduce_scatter | solution.py:73
  585.8 0.0 copy-done.1
  585.8 2.2 add_convert_fusion.1
  588.0 199.8 %reduce-scatter.5.cloned.1.call-done = bf16[1024,2752]{0,1:T(8,128)(2,1)} async-done(((bf16[4096,2752]{0,1:T(8,128)(2,1)}), bf16[1024,2752]{0,1:T(8,128)(2,1)}) %reduce-scatter.5.cloned.1.call-update) | async-done | bytes 5636112 | tf_op jit(solution)/shard_map/reduce_scatter | solution.py:85
  787.8 8.3 %fusion.39 = (f32[1024,1376]{0,1:T(8,128)}, f32[1024,1376]{0,1:T(8,128)}) fusion(bf16[1024,2752]{0,1:T(8,128)(2,1)} %reduce-scatter.5.cloned.1.call-done), kind=kLoop, calls=%fused_computation.62 | loop fusion | bytes 22544384 | tf_op jit(solution)/shard_map/slice | solution.py:91
  (10 shorter events, 0.0 us)
Async XLA Ops:
  7.2 214.6 %all-gather.5.cloned.1.call-start = ((), (), s32[]{:S(2)}) async-start(), calls=%async_computation.2 | async-start | bytes 28180480 | tf_op jit(solution)/shard_map/all_gather | solution.py:65
  12.9 0.7 copy-start.10
  12.9 0.8 copy-start.4
  12.9 1.2 copy-start
  12.9 3.6 copy-start.2
  12.9 208.9 %copy-start.6 = (bf16[768,1376]{0,1:T(8,128)(2,1)S(1)}, bf16[768,1376]{0,1:T(8,128)(2,1)}, u32[]{:S(2)}) copy-start(bf16[768,1376]{0,1:T(8,128)(2,1)} %param.15) | copy-start | bytes 6340612
  12.9 275.8 %all-gather.7.cloned.1.call-start = ((), (), s32[]{:S(2)}) async-start(), calls=%async_computation.4 | async-start | bytes 7077888 | tf_op jit(solution)/shard_map/all_gather | solution.py:59
  15.2 385.5 %all-gather.9.cloned.1.call-start = ((), (), s32[]{:S(2)}) async-start(), calls=%async_computation.5 | async-start | bytes 14090240 | tf_op jit(solution)/shard_map/all_gather | solution.py:70
  15.9 498.0 %all-gather.11.cloned.1.call-start = ((), (), s32[]{:S(2)}) async-start(), calls=%async_computation.6 | async-start | bytes 14090240 | tf_op jit(solution)/shard_map/all_gather | solution.py:71
  16.5 569.3 %reduce-scatter.3.cloned.1.call-start = ((), (), s32[]{:S(2)}) async-start(), calls=%async_computation.3 | async-start | bytes 7077888 | tf_op jit(solution)/shard_map/reduce_scatter | solution.py:73
  221.8 18.6 %copy-start.7 = (bf16[768,1376]{0,1:T(8,128)(2,1)S(1)}, bf16[768,1376]{0,1:T(8,128)(2,1)}, u32[]{:S(2)}) copy-start(bf16[768,1376]{0,1:T(8,128)(2,1)} %param.14) | copy-start | bytes 6340612
  258.7 0.7 copy-start.3
  258.7 30.0 %copy-start.8 = (bf16[768,1376]{0,1:T(8,128)(2,1)S(1)}, bf16[768,1376]{0,1:T(8,128)(2,1)}, u32[]{:S(2)}) copy-start(bf16[768,1376]{0,1:T(8,128)(2,1)} %param.20) | copy-start | bytes 6340612
  258.7 529.1 %reduce-scatter.5.cloned.1.call-start = ((), (), s32[]{:S(2)}) async-start(), calls=%async_computation.7 | async-start | bytes 28180480 | tf_op jit(solution)/shard_map/reduce_scatter | solution.py:85
  288.7 15.3 %copy-start.5 = (bf16[768,4096]{1,0:T(8,128)(2,1)S(1)}, bf16[768,4096]{1,0:T(8,128)(2,1)}, u32[]{:S(2)}) copy-start(bf16[768,4096]{1,0:T(8,128)(2,1)} %all-gather.7.cloned.1.call-done) | copy-start | bytes 18874372
  288.7 15.3 %copy-start.9 = (bf16[768,1376]{0,1:T(8,128)(2,1)S(1)}, bf16[768,1376]{0,1:T(8,128)(2,1)}, u32[]{:S(2)}) copy-start(bf16[768,1376]{0,1:T(8,128)(2,1)} %param.21) | copy-start | bytes 6340612
  415.8 170.1 %copy-start.1 = (bf16[768,512]{1,0:T(8,128)(2,1)S(1)}, bf16[768,512]{1,0:T(8,128)(2,1)}, u32[]{:S(2)}) copy-start(bf16[768,512]{1,0:T(8,128)(2,1)} %param.16) | copy-start | bytes 2359300
Sparse Core Ops, SparseCore 0:
  13.0 208.7 all-gather.4
  224.0 64.6 all-gather.6
  290.5 110.1 all-gather.8
  402.4 111.4 all-gather.10
  516.0 69.7 reduce-scatter.2
  588.8 198.9 reduce-scatter.4
where the time goes:
time: 803 us
  waiting for transfers between devices  652 us (81%)
  matrix products  97 us (12%)
  other arithmetic  29.2 us (4%)
  between operations  14.2 us (2%)
  local copies, waits for them, and re-layouts  9.76 us (1%)
    all_gather x1, waiting for transfers between devices, per_device(): piece = lax.all_gather(stacked_ref, 'fsdp', axis=1, tiled=True)  205 us
    reduce_scatter x1, waiting for transfers between devices, per_device(): lax.psum_scatter(jnp.concatenate([term_text, term_image], axis=1).astype(...  200 us
    all_gather x1, waiting for transfers between devices, per_device(): lax.all_gather(pol_down_image, 'fsdp', axis=0, tiled=True)  98.1 us
    all_gather x1, waiting for transfers between devices, per_device(): lax.all_gather(pol_down_text, 'fsdp', axis=0, tiled=True)  64.2 us
    reduce_scatter x1, waiting for transfers between devices, per_device(): lax.psum_scatter(terms.astype(jnp.bfloat16), 'tp', scatter_dimension=1, t...  54.4 us
    all_gather x1, waiting for transfers between devices, per_device(): full_cot = lax.all_gather(local_cot, 'tp', axis=1, tiled=True)  29.3 us
    concatenate x1, other arithmetic, per_device(): jnp.concatenate([term_text, term_image], axis=1).astype(jnp.bfloat16)  20.2 us
    dot_general x1, matrix products, forward_term(): lax.dot_general(left_image, right_image, contract, preferred_element_type...  18.6 us
  transfers between devices with their start and end apart: 6, of which 6 were waited for; matrix products, arithmetic and copies ran while one was open for 15% of the time, Pallas kernels for 0%

commit v1 on v0

v1 whole, which is shorter than its diff:
```python
import jax
import jax.numpy as jnp
from jax import lax
from jax.sharding import PartitionSpec as P


dpo_beta = 0.1


def silu_parts(gate, up):
    gate_f = gate.astype(jnp.float32)
    up_f = up.astype(jnp.float32)
    sig = jax.nn.sigmoid(gate_f)
    act = gate_f * sig
    return gate_f, up_f, sig, act


def hidden_of(gate, up):
    _, up_f, _, act = silu_parts(gate, up)
    return (act * up_f).astype(jnp.bfloat16)


def swap_pairs(n_fsdp, n_tp):
    r = n_tp // n_fsdp
    return [
        (f * n_tp + q * r + j, q * n_tp + f * r + j)
        for f in range(n_fsdp)
        for q in range(n_fsdp)
        for j in range(r)
    ]


def gather_modality(ref_modality, pol_modality, n_fsdp):
    own = jnp.stack([ref_modality, pol_modality])
    me = lax.axis_index("fsdp")
    both = jnp.zeros((n_fsdp,) + own.shape, own.dtype)
    both = lax.dynamic_update_index_in_dim(both, own, me, 0)
    for s in range(1, n_fsdp):
        got = lax.ppermute(own, "fsdp", [(i, (i + s) % n_fsdp) for i in range(n_fsdp)])
        both = lax.dynamic_update_index_in_dim(both, got, (me - s) % n_fsdp, 0)
    return both[:, 0].reshape(-1), both[:, 1].reshape(-1)


def per_device(
    n_fsdp,
    n_tp,
    ref_gate,
    ref_up,
    ref_residual,
    ref_modality,
    ref_down_text,
    ref_down_image,
    pol_gate,
    pol_up,
    pol_modality,
    pol_segment,
    pair_margin,
    token_cotangent,
    pol_down_text,
    pol_down_image,
):
    rows, feats = token_cotangent.shape
    pairs = swap_pairs(n_fsdp, n_tp)
    partner = [(t, t ^ 1) for t in range(n_tp)]
    index = lax.axis_index("tp")
    line, half = index // 2, index % 2

    def shift(step):
        return [(t, (t + 2 * step) % n_tp) for t in range(n_tp)]

    seg_ids = jnp.arange(2 * pair_margin.shape[0], dtype=jnp.int32)
    pair_weight = dpo_beta * jax.nn.sigmoid(-dpo_beta * pair_margin)
    table = jnp.repeat(pair_weight, 2) * jnp.where(seg_ids % 2 == 0, -1.0, 1.0).astype(jnp.float32)
    coef = jnp.sum(
        jnp.where(pol_segment[:, None] == seg_ids[None, :], table[None, :], jnp.float32(0.0)),
        axis=1,
    )
    pol_own = hidden_of(pol_gate, pol_up)
    pol_hidden = lax.all_gather(pol_own, "fsdp", axis=0, tiled=True)
    ref_own = hidden_of(ref_gate, ref_up)
    ref_hidden = lax.all_gather(ref_own, "fsdp", axis=0, tiled=True)

    local_cot = (coef[:, None] * token_cotangent.astype(jnp.float32)).astype(jnp.bfloat16)
    moved = lax.ppermute(local_cot, ("fsdp", "tp"), pairs)
    modality_r, modality_p = gather_modality(ref_modality, pol_modality, n_fsdp)
    image_r = (modality_r == 1)[:, None]
    image_p = (modality_p == 1)[:, None]

    mine = jnp.zeros((n_fsdp, rows, feats), jnp.bfloat16)
    mine = lax.dynamic_update_index_in_dim(mine, moved, line, 0)
    for s in range(1, n_fsdp):
        got = lax.ppermute(moved, "tp", shift(s))
        mine = lax.dynamic_update_index_in_dim(mine, got, (line - s) % n_fsdp, 0)
    mine = mine.reshape(n_fsdp * rows, feats)
    theirs = lax.ppermute(mine, "tp", partner)
    first = half == 0
    cot_full = jnp.concatenate(
        [jnp.where(first, mine, theirs), jnp.where(first, theirs, mine)], axis=1
    )

    dh_text = jnp.dot(cot_full, pol_down_text, preferred_element_type=jnp.float32)
    dh_image = jnp.dot(cot_full, pol_down_image, preferred_element_type=jnp.float32)
    dh_part = jnp.where(image_p, dh_image, dh_text).astype(jnp.bfloat16)
    d_hidden = lax.psum_scatter(dh_part, "fsdp", scatter_dimension=0, tiled=True)

    zero = jnp.zeros_like(cot_full)
    over_rows = (((0,), (0,)), ((), ()))
    g_text = lax.dot_general(
        jnp.where(image_p, zero, cot_full), pol_hidden, over_rows, preferred_element_type=jnp.float32
    )
    g_image = lax.dot_general(
        jnp.where(image_p, cot_full, zero), pol_hidden, over_rows, preferred_element_type=jnp.float32
    )

    contract = (((1,), (1,)), ((), ()))

    def out_half(which):
        w_text = lax.dynamic_slice_in_dim(ref_down_text, which * feats, feats, 0)
        w_image = lax.dynamic_slice_in_dim(ref_down_image, which * feats, feats, 0)
        o_text = lax.dot_general(ref_hidden, w_text, contract, preferred_element_type=jnp.float32)
        o_image = lax.dot_general(ref_hidden, w_image, contract, preferred_element_type=jnp.float32)
        return jnp.where(image_r, o_image, o_text).astype(jnp.bfloat16)

    got = lax.ppermute(out_half(1 - half), "tp", partner)
    keep = out_half(half)
    both = (keep.astype(jnp.float32) + got.astype(jnp.float32)).astype(jnp.bfloat16)
    both = both.reshape(n_fsdp, rows, feats)
    total = lax.dynamic_index_in_dim(both, line, 0, keepdims=False).astype(jnp.float32)
    for s in range(1, n_fsdp):
        piece = lax.dynamic_index_in_dim(both, (line + s) % n_fsdp, 0, keepdims=False)
        total = total + lax.ppermute(piece, "tp", shift(s)).astype(jnp.float32)
    summed = lax.ppermute(total.astype(jnp.bfloat16), ("fsdp", "tp"), pairs)
    ref_out = (summed.astype(jnp.float32) + ref_residual.astype(jnp.float32)).astype(jnp.bfloat16)

    late_gate, late_up, d_hidden = lax.optimization_barrier((pol_gate, pol_up, d_hidden))
    gate_f, up_f, sig, act = silu_parts(late_gate, late_up)
    d_hidden = d_hidden.astype(jnp.float32)
    grad_gate = (d_hidden * up_f * sig * (1.0 + gate_f * (1.0 - sig))).astype(jnp.bfloat16)
    grad_up = (d_hidden * act).astype(jnp.bfloat16)
    return (ref_out, grad_gate, grad_up, g_text, g_image)


def solution(mesh):
    n_fsdp, n_tp = mesh.shape["fsdp"], mesh.shape["tp"]
    two = P("fsdp", "tp")
    one = P("fsdp")
    in_specs = (two, two, two, one, two, two, two, two, one, one, P(), two, two, two)

    def body(*args):
        return per_device(n_fsdp, n_tp, *args)

    return jax.shard_map(
        body, mesh=mesh, in_specs=in_specs, out_specs=(two,) * 5, check_vma=False
    )
```

time: 803 us -> 380 us (0.47)
  the two profiles are of different devices: /device:TPU:0 before, /device:TPU:28 now
where the time goes in v1:
time: 380 us; the launch traced here: 376 us
  waiting for transfers between devices  192 us (51%)
  matrix products  87.7 us (23%)
  starting transfers between devices  44.5 us (12%)
  other arithmetic  22.7 us (6%)
  local copies, waits for them, and re-layouts  14.7 us (4%)
  between operations  14.3 us (4%)
    ppermute x1, waiting for transfers between devices, per_device(): moved = lax.ppermute(local_cot, ('fsdp', 'tp'), pairs)  52.9 us
    ppermute x3, waiting for transfers between devices, per_device(): total = total + lax.ppermute(piece, 'tp', shift(s)).astype(jnp.float32)  49.6 us
    ppermute x3, waiting for transfers between devices, per_device(): got = lax.ppermute(moved, 'tp', shift(s))  46 us
    ppermute x1, waiting for transfers between devices, per_device(): summed = lax.ppermute(total.astype(jnp.bfloat16), ('fsdp', 'tp'), pairs)  41.9 us
    ppermute x3, starting transfers between devices, gather_modality(): lax.ppermute(own, 'fsdp', [(i, (i + s) % n_fsdp) for i in range(n_fsdp)])  31.9 us
    dot_general x2, matrix products, out_half(): lax.dot_general(ref_hidden, w_image, contract, preferred_element_type=jnp...  18.6 us
    dot_general x1, matrix products, per_device(): lax.dot_general(jnp.where(image_p, cot_full, zero), pol_hidden, over_rows...  17.1 us
    dot_general x2, matrix products, out_half(): lax.dot_general(ref_hidden, w_text, contract, preferred_element_type=jnp....  16.1 us
  transfers between devices with their start and end apart: 16, of which 6 were waited for; matrix products, arithmetic and copies ran while one was open for 30% of the time, Pallas kernels for 0%

profile of v1, /device:TPU:28, one launch (start us, length us, event | category | flops | bytes accessed | tf_op | source)
XLA Modules:
  0.0 375.5 jit_solution(16656419969737095516)
XLA Ops:
  7.2 0.0 all-gather.3.cloned.1.call-start
  7.2 5.0 %fusion.23 = bf16[768,1376]{0,1:T(8,128)(2,1)} fusion(bf16[768,1376]{0,1:T(8,128)(2,1)} %param.15, bf16[768,1376]{0,1:T(8,128)(2,1)} %param.14), kind=kLoop, calls=%fused_computation.37 | loop fusion | flops 8454144 | bytes 6340608 | tf_op jit(solution)/shard_map/convert_element_type | solution.py:20
  12.3 0.0 all-gather.5.cloned.1.call-start
  12.3 4.8 %fusion.22 = bf16[768,1376]{0,1:T(8,128)(2,1)} fusion(bf16[768,1376]{0,1:T(8,128)(2,1)} %param.21, bf16[768,1376]{0,1:T(8,128)(2,1)} %param.20), kind=kLoop, calls=%fused_computation.36 | loop fusion | flops 8454144 | bytes 6340608 | tf_op jit(solution)/shard_map/convert_element_type | solution.py:20
  17.2 0.0 reduce-scatter.2.cloned.1.call-start
  17.2 0.1 broadcast_in_dim.102
  17.3 0.1 reshape.54
  17.4 0.1 select_reduce_fusion
  17.5 1.4 multiply_convert_fusion
  18.9 3.3 collective-permute-start.8
  22.2 52.9 %collective-permute-done.8 = bf16[768,512]{1,0:T(8,128)(2,1)} collective-permute-done((bf16[768,512]{1,0:T(8,128)(2,1)S(1)}, bf16[768,512]{1,0:T(8,128)(2,1)}, u32[]{:S(2)}, u32[]{:S(2)}) %collective-permute-start.8) | collective-permute-done | bytes 786464 | tf_op jit(solution)/shard_map/ppermute | solution.py:84
  75.0 1.0 collective-permute-start.9
  76.0 1.0 collective-permute-start.11
  77.1 1.9 broadcast_in_dim.101
  79.0 2.1 bitcast_dynamic-update-slice_fusion.3
  81.1 27.2 %collective-permute-done.9 = bf16[768,512]{1,0:T(8,128)(2,1)} collective-permute-done((bf16[768,512]{1,0:T(8,128)(2,1)}, bf16[768,512]{1,0:T(8,128)(2,1)}, u32[]{:S(2)}, u32[]{:S(2)}) %collective-permute-start.9) | collective-permute-done | bytes 786464 | tf_op jit(solution)/shard_map/ppermute | solution.py:92
  108.2 2.1 bitcast_dynamic-update-slice_fusion.2
  110.3 18.8 %collective-permute-done.10 = bf16[768,512]{1,0:T(8,128)(2,1)} collective-permute-done((bf16[768,512]{1,0:T(8,128)(2,1)}, bf16[768,512]{1,0:T(8,128)(2,1)}, u32[]{:S(2)}, u32[]{:S(2)}) %collective-permute-start.10) | collective-permute-done | bytes 786464 | tf_op jit(solution)/shard_map/ppermute | solution.py:92
  129.1 2.1 bitcast_dynamic-update-slice_fusion.1
  131.2 0.9 bitcast_dynamic-update-slice_fusion
  132.2 14.8 %collective-permute-start = (s32[2,768]{1,0:T(2,128)S(1)}, s32[2,768]{1,0:T(2,128)S(1)}, u32[]{:S(2)}, u32[]{:S(2)}) collective-permute-start(s32[2,768]{1,0:T(2,128)S(1)} %get-tuple-element.20), channel_id=1, source_target_pairs={{0,8},{8,16},{16,24},{24,0},{1,9},{9,17},{17,25},{25,1},{2,10},{10... | collective-permute-start | bytes 18440 | tf_op jit(solution)/shard_map/ppermute | solution.py:39
  146.9 14.3 %collective-permute-start.1 = (s32[2,768]{1,0:T(2,128)S(1)}, s32[2,768]{1,0:T(2,128)S(1)}, u32[]{:S(2)}, u32[]{:S(2)}) collective-permute-start(s32[2,768]{1,0:T(2,128)S(1)} %get-tuple-element.20), channel_id=1, source_target_pairs={{0,16},{8,24},{16,0},{24,8},{1,17},{9,25},{17,1},{25,9},{2,18},{10... | collective-permute-start | bytes 18440 | tf_op jit(solution)/shard_map/ppermute | solution.py:39
  161.2 2.8 collective-permute-start.2
  164.1 0.1 dynamic_update_slice.26
  164.2 0.1 dynamic_update_slice.27
  164.3 0.1 dynamic_update_slice.28
  164.4 1.1 collective-permute-done.2
  165.5 0.3 dynamic_update_slice.29
  165.9 3.3 broadcast_select_fusion.1
  169.2 11.1 %fusion.43 = bf16[3072,1376]{0,1:T(8,128)(2,1)} fusion(bf16[1024,1376]{0,1:T(8,128)(2,1)S(1)} %copy-done, bf16[3072,512]{1,0:T(8,128)(2,1)S(1)} %get-tuple-element.12, bf16[3072,512]{1,0:T(8,128)(2,1)S(1)} %get-tuple-element.11), kind=kOutput, calls=%fused_computation.77 | convolution fusion | flops 8669626368 | bytes 17563648 | tf_op jit(solution)/shard_map/dot_general | solution.py:101
  180.3 13.0 %select_convert_fusion = bf16[3072,1376]{0,1:T(8,128)(2,1)} fusion(bf16[3072,1376]{0,1:T(8,128)(2,1)} %fusion.43, bf16[1024,1376]{0,1:T(8,128)(2,1)S(1)} %copy-done.13, pred[3072]{0:T(1024)(128)(4,1)S(1)} %eq.59, bf16[3072,512]{1,0:T(8,128)(2,1)S(1)} %get-tuple-element.12, bf16[3072,512]{1,0:T(8,128)(2,1)S(1)} %get-tuple-element.11), kind=kOutput, calls=%fused_computation | convolution fusion | flops 8673853440 | bytes 26020864 | tf_op jit(solution)/shard_map/dot_general | solution.py:102
  193.4 1.7 copy-done.14
  195.1 9.0 %fusion.30 = bf16[3072,512]{1,0:T(8,128)(2,1)S(1)} fusion(bf16[3072,1376]{0,1:T(8,128)(2,1)} %all-gather.3.cloned.1.call-done, bf16[1024,1376]{0,1:T(8,128)(2,1)S(1)} %copy-done.14, s32[]{:T(128)S(6)} %select_n.154), kind=kOutput, calls=%fused_computation.49 | convolution fusion | flops 4328521728 | bytes 13008900 | tf_op jit(solution)/shard_map/dot_general | solution.py:121
  204.1 7.3 %select_convert_fusion.1 = bf16[3072,512]{1,0:T(8,128)(2,1)} fusion(bf16[3072,512]{1,0:T(8,128)(2,1)S(1)} %fusion.30, bf16[3072,1376]{0,1:T(8,128)(2,1)S(1)} %copy-done.12, pred[3072]{0:T(1024)(128)(4,1)S(1)} %eq.57, bf16[1024,1376]{0,1:T(8,128)(2,1)S(1)} %copy-done.15, s32[]{:T(128)S(6)} %select_n.154), kind=kOutput, calls=%fused_computation.10 | convolution fusion | flops 4330094592 | bytes 16157700 | tf_op jit(solution)/shard_map/dot_general | solution.py:120
  211.4 9.6 %fusion.33 = bf16[3072,512]{1,0:T(8,128)(2,1)S(1)} fusion(bf16[3072,1376]{0,1:T(8,128)(2,1)} %all-gather.3.cloned.1.call-done, bf16[1024,1376]{0,1:T(8,128)(2,1)S(1)} %copy-done.14, s32[]{:T(128)S(6)} %select_n.152), kind=kOutput, calls=%fused_computation.52 | convolution fusion | flops 4328521728 | bytes 13008900 | tf_op jit(solution)/shard_map/dot_general | solution.py:121
  221.1 8.8 %add_convert_fusion = bf16[3072,512]{1,0:T(8,128)(2,1)S(1)} fusion(bf16[3072,512]{1,0:T(8,128)(2,1)} %collective-permute-done.3, bf16[3072,512]{1,0:T(8,128)(2,1)S(1)} %fusion.33, bf16[3072,1376]{0,1:T(8,128)(2,1)} %all-gather.3.cloned.1.call-done, pred[3072]{0:T(1024)(128)(4,1)S(1)} %eq.57, bf16[1024,1376]{0,1:T(8,128)(2,1)S(1)} %copy-done.16, ...), kind=kOutput, calls=%fused_computation.9 | convolution fusion | flops 4336386048 | bytes 19303428 | tf_op jit(solution)/shard_map/dot_general | solution.py:120
  229.9 1.7 copy-done.6
  231.6 1.4 dynamic-slice_bitcast_fusion.2
  233.0 2.7 collective-permute-start.5
  235.7 2.2 collective-permute-start.6
  237.9 17.1 %fusion = f32[1024,1376]{0,1:T(8,128)} fusion(bf16[3072,1376]{0,1:T(8,128)(2,1)} %all-gather.5.cloned.1.call-done, pred[3072]{0:T(1024)(128)(4,1)S(1)} %eq.59, bf16[3072,512]{1,0:T(8,128)(2,1)} %copy-done.4, bf16[3072,512]{1,0:T(8,128)(2,1)} %copy-done.2), kind=kOutput, calls=%fused_computation.5 | convolution fusion | flops 8672772096 | bytes 20384768 | tf_op jit(solution)/shard_map/dot_general | solution.py:111
  255.0 49.6 %collective-permute-done.5 = bf16[768,512]{1,0:T(8,128)(2,1)S(1)} collective-permute-done((bf16[768,512]{1,0:T(8,128)(2,1)}, bf16[768,512]{1,0:T(8,128)(2,1)S(1)}, u32[]{:S(2)}, u32[]{:S(2)}) %collective-permute-start.5) | collective-permute-done | bytes 786464 | tf_op jit(solution)/shard_map/ppermute | solution.py:131
  304.6 1.5 fusion.28
  306.2 2.3 collective-permute-start.7
  308.5 11.7 %fusion.2 = f32[1024,1376]{0,1:T(8,128)} fusion(bf16[3072,1376]{0,1:T(8,128)(2,1)S(1)} %copy-done.11, pred[3072]{0:T(1024)(128)(4,1)S(1)} %eq.59, bf16[3072,512]{1,0:T(8,128)(2,1)S(1)} %copy-done.5, bf16[3072,512]{1,0:T(8,128)(2,1)S(1)} %copy-done.3), kind=kOutput, calls=%fused_computation.7 | convolution fusion | flops 8672772096 | bytes 20384768 | tf_op jit(solution)/shard_map/dot_general | solution.py:108
  320.2 41.9 %collective-permute-done.7 = bf16[768,512]{1,0:T(8,128)(2,1)S(1)} collective-permute-done((bf16[768,512]{1,0:T(8,128)(2,1)S(1)}, bf16[768,512]{1,0:T(8,128)(2,1)S(1)}, u32[]{:S(2)}, u32[]{:S(2)}) %collective-permute-start.7) | collective-permute-done | bytes 786464 | tf_op jit(solution)/shard_map/ppermute | solution.py:132
  362.1 1.1 add_convert_fusion.1
  363.3 5.5 %fusion.13 = (bf16[768,1376]{0,1:T(8,128)(2,1)}, bf16[768,1376]{0,1:T(8,128)(2,1)}) fusion(bf16[768,1376]{0,1:T(8,128)(2,1)} %reduce-scatter.2.cloned.1.call-done, bf16[768,1376]{0,1:T(8,128)(2,1)} %param.20, bf16[768,1376]{0,1:T(8,128)(2,1)} %param.21), kind=kLoop, calls=%fused_computation.27 | loop fusion | flops 16908288 | bytes 10567680 | tf_op jit(solution)/shard_map/convert_element_type | solution.py:139
  (64 shorter events, 0.3 us)
Async XLA Ops:
  7.2 162.0 %copy-start = (bf16[1024,1376]{0,1:T(8,128)(2,1)S(1)}, bf16[1024,1376]{0,1:T(8,128)(2,1)}, u32[]{:S(2)}) copy-start(bf16[1024,1376]{0,1:T(8,128)(2,1)} %param.26) | copy-start | bytes 8454148
  7.2 186.2 %all-gather.3.cloned.1.call-start = ((), (), s32[]{:S(2)}) async-start(), calls=%async_computation.1 | async-start | bytes 10567680 | tf_op jit(solution)/shard_map/all_gather | solution.py:81
  12.2 5.0 %copy-start.17 = (f32[3]{0:T(128)S(1)}, f32[3]{0:T(128)}, u32[]{:S(2)}) copy-start(f32[3]{0:T(128)} %param.24) | copy-start | bytes 40
  12.2 5.2 %copy-start.10 = (s32[768]{0:T(1024)S(1)}, s32[768]{0:T(1024)}, u32[]{:S(2)}) copy-start(s32[768]{0:T(1024)} %param.23) | copy-start | bytes 9220
  12.3 225.6 %all-gather.5.cloned.1.call-start = ((), (), s32[]{:S(2)}) async-start(), calls=%async_computation.3 | async-start | bytes 10567680 | tf_op jit(solution)/shard_map/all_gather | solution.py:79
  17.2 346.1 %reduce-scatter.2.cloned.1.call-start = ((), (), s32[]{:S(2)}) async-start(), calls=%async_computation.2 | async-start | bytes 10567680 | tf_op jit(solution)/shard_map/reduce_scatter | solution.py:104
  18.9 56.2 %collective-permute-start.8 = (bf16[768,512]{1,0:T(8,128)(2,1)S(1)}, bf16[768,512]{1,0:T(8,128)(2,1)}, u32[]{:S(2)}, u32[]{:S(2)}) collective-permute-start(bf16[768,512]{1,0:T(8,128)(2,1)S(1)} %multiply_convert_fusion), channel_id=1, source_target_pairs={{0,0},{1,1},{2,8},{3,9},{4,16},{5,17},{6,24},{7,25},{8,2},{9,3},{1... | collective-permute-start | bytes 2359304 | tf_op jit(solution)/shard_map/ppermute | solution.py:84
  75.0 33.2 %collective-permute-start.9 = (bf16[768,512]{1,0:T(8,128)(2,1)}, bf16[768,512]{1,0:T(8,128)(2,1)}, u32[]{:S(2)}, u32[]{:S(2)}) collective-permute-start(bf16[768,512]{1,0:T(8,128)(2,1)} %collective-permute-done.8), channel_id=1, source_target_pairs={{0,2},{1,3},{2,4},{3,5},{4,6},{5,7},{6,0},{7,1},{8,10},{9,11},{10,... | collective-permute-start | bytes 2359304 | tf_op jit(solution)/shard_map/ppermute | solution.py:92
  76.0 53.1 %collective-permute-start.10 = (bf16[768,512]{1,0:T(8,128)(2,1)}, bf16[768,512]{1,0:T(8,128)(2,1)}, u32[]{:S(2)}, u32[]{:S(2)}) collective-permute-start(bf16[768,512]{1,0:T(8,128)(2,1)} %collective-permute-done.8), channel_id=1, source_target_pairs={{0,4},{1,5},{2,6},{3,7},{4,0},{5,1},{6,2},{7,3},{8,12},{9,13},{10,... | collective-permute-start | bytes 2359304 | tf_op jit(solution)/shard_map/ppermute | solution.py:92
  76.0 55.2 %collective-permute-start.11 = (bf16[768,512]{1,0:T(8,128)(2,1)}, bf16[768,512]{1,0:T(8,128)(2,1)S(1)}, u32[]{:S(2)}, u32[]{:S(2)}) collective-permute-start(bf16[768,512]{1,0:T(8,128)(2,1)} %collective-permute-done.8), channel_id=1, source_target_pairs={{0,6},{1,7},{2,0},{3,1},{4,2},{5,3},{6,4},{7,5},{8,14},{9,15},{10,... | collective-permute-start | bytes 2359304 | tf_op jit(solution)/shard_map/ppermute | solution.py:92
  79.0 53.1 %copy-start.8 = (s32[768]{0:T(1024)S(1)}, s32[768]{0:T(1024)}, u32[]{:S(2)}) copy-start(s32[768]{0:T(1024)} %param.22) | copy-start | bytes 9220
  79.0 53.2 %copy-start.9 = (s32[768]{0:T(1024)S(1)}, s32[768]{0:T(1024)}, u32[]{:S(2)}) copy-start(s32[768]{0:T(1024)} %param.17) | copy-start | bytes 9220
  132.1 33.7 %collective-permute-start.12 = (bf16[3072,512]{1,0:T(8,128)(2,1)}, bf16[3072,512]{1,0:T(8,128)(2,1)}, u32[]{:S(2)}, u32[]{:S(2)}) collective-permute-start(bf16[3072,512]{1,0:T(8,128)(2,1)} %bitcast.12), channel_id=1, source_target_pairs={{0,1},{1,0},{2,3},{3,2},{4,5},{5,4},{6,7},{7,6},{8,9},{9,8},{10,11... | collective-permute-start | bytes 9437192 | tf_op jit(solution)/shard_map/ppermute | solution.py:95
  132.2 32.0 %collective-permute-start = (s32[2,768]{1,0:T(2,128)S(1)}, s32[2,768]{1,0:T(2,128)S(1)}, u32[]{:S(2)}, u32[]{:S(2)}) collective-permute-start(s32[2,768]{1,0:T(2,128)S(1)} %get-tuple-element.20), channel_id=1, source_target_pairs={{0,8},{8,16},{16,24},{24,0},{1,9},{9,17},{17,25},{25,1},{2,10},{10... | collective-permute-start | bytes 18440 | tf_op jit(solution)/shard_map/ppermute | solution.py:39
  146.9 17.3 %collective-permute-start.1 = (s32[2,768]{1,0:T(2,128)S(1)}, s32[2,768]{1,0:T(2,128)S(1)}, u32[]{:S(2)}, u32[]{:S(2)}) collective-permute-start(s32[2,768]{1,0:T(2,128)S(1)} %get-tuple-element.20), channel_id=1, source_target_pairs={{0,16},{8,24},{16,0},{24,8},{1,17},{9,25},{17,1},{25,9},{2,18},{10... | collective-permute-start | bytes 18440 | tf_op jit(solution)/shard_map/ppermute | solution.py:39
  161.2 4.2 %collective-permute-start.2 = (s32[2,768]{1,0:T(2,128)S(1)}, s32[2,768]{1,0:T(2,128)S(1)}, u32[]{:S(2)}, u32[]{:S(2)}) collective-permute-start(s32[2,768]{1,0:T(2,128)S(1)} %get-tuple-element.20), channel_id=1, source_target_pairs={{0,24},{8,0},{16,8},{24,16},{1,25},{9,1},{17,9},{25,17},{2,26},{10... | collective-permute-start | bytes 18440 | tf_op jit(solution)/shard_map/ppermute | solution.py:39
  169.1 11.2 %copy-start.2 = (bf16[3072,512]{1,0:T(8,128)(2,1)}, bf16[3072,512]{1,0:T(8,128)(2,1)S(1)}, u32[]{:S(2)}) copy-start(bf16[3072,512]{1,0:T(8,128)(2,1)S(1)} %get-tuple-element.11) | copy-start | bytes 9437188
  169.2 11.2 %copy-start.4 = (bf16[3072,512]{1,0:T(8,128)(2,1)}, bf16[3072,512]{1,0:T(8,128)(2,1)S(1)}, u32[]{:S(2)}) copy-start(bf16[3072,512]{1,0:T(8,128)(2,1)S(1)} %get-tuple-element.12) | copy-start | bytes 9437188
  169.2 11.2 %copy-start.13 = (bf16[1024,1376]{0,1:T(8,128)(2,1)S(1)}, bf16[1024,1376]{0,1:T(8,128)(2,1)}, u32[]{:S(2)}) copy-start(bf16[1024,1376]{0,1:T(8,128)(2,1)} %param.27) | copy-start | bytes 8454148
  193.3 1.8 copy-start.14
  195.1 9.0 %copy-start.12 = (bf16[3072,1376]{0,1:T(8,128)(2,1)S(1)}, bf16[3072,1376]{0,1:T(8,128)(2,1)}, u32[]{:S(2)}) copy-start(bf16[3072,1376]{0,1:T(8,128)(2,1)} %all-gather.3.cloned.1.call-done) | copy-start | bytes 25362436
  195.1 9.0 %copy-start.15 = (bf16[1024,1376]{0,1:T(8,128)(2,1)S(1)}, bf16[1024,1376]{0,1:T(8,128)(2,1)}, u32[]{:S(2)}) copy-start(bf16[1024,1376]{0,1:T(8,128)(2,1)} %param.18) | copy-start | bytes 8454148
  211.4 9.6 %collective-permute-start.3 = (bf16[3072,512]{1,0:T(8,128)(2,1)}, bf16[3072,512]{1,0:T(8,128)(2,1)}, u32[]{:S(2)}, u32[]{:S(2)}) collective-permute-start(bf16[3072,512]{1,0:T(8,128)(2,1)} %select_convert_fusion.1), channel_id=1, source_target_pairs={{0,1},{1,0},{2,3},{3,2},{4,5},{5,4},{6,7},{7,6},{8,9},{9,8},{10,11... | collective-permute-start | bytes 9437192 | tf_op jit(solution)/shard_map/ppermute | solution.py:124
  211.4 9.6 %copy-start.16 = (bf16[1024,1376]{0,1:T(8,128)(2,1)S(1)}, bf16[1024,1376]{0,1:T(8,128)(2,1)}, u32[]{:S(2)}) copy-start(bf16[1024,1376]{0,1:T(8,128)(2,1)} %param.18) | copy-start | bytes 8454148
  229.9 1.7 copy-start.6
  233.0 22.0 %collective-permute-start.4 = (bf16[768,512]{1,0:T(8,128)(2,1)}, bf16[768,512]{1,0:T(8,128)(2,1)S(1)}, u32[]{:S(2)}, u32[]{:S(2)}) collective-permute-start(bf16[768,512]{1,0:T(8,128)(2,1)} %get-tuple-element.15), channel_id=1, source_target_pairs={{0,2},{1,3},{2,4},{3,5},{4,6},{5,7},{6,0},{7,1},{8,10},{9,11},{10,... | collective-permute-start | bytes 2359304 | tf_op jit(solution)/shard_map/ppermute | solution.py:131
  233.0 71.6 %collective-permute-start.5 = (bf16[768,512]{1,0:T(8,128)(2,1)}, bf16[768,512]{1,0:T(8,128)(2,1)S(1)}, u32[]{:S(2)}, u32[]{:S(2)}) collective-permute-start(bf16[768,512]{1,0:T(8,128)(2,1)} %get-tuple-element.17), channel_id=1, source_target_pairs={{0,4},{1,5},{2,6},{3,7},{4,0},{5,1},{6,2},{7,3},{8,12},{9,13},{10,... | collective-permute-start | bytes 2359304 | tf_op jit(solution)/shard_map/ppermute | solution.py:131
  235.7 68.9 %collective-permute-start.6 = (bf16[768,512]{1,0:T(8,128)(2,1)}, bf16[768,512]{1,0:T(8,128)(2,1)S(1)}, u32[]{:S(2)}, u32[]{:S(2)}) collective-permute-start(bf16[768,512]{1,0:T(8,128)(2,1)} %get-tuple-element.16), channel_id=1, source_target_pairs={{0,6},{1,7},{2,0},{3,1},{4,2},{5,3},{6,4},{7,5},{8,14},{9,15},{10,... | collective-permute-start | bytes 2359304 | tf_op jit(solution)/shard_map/ppermute | solution.py:131
  237.9 70.6 %copy-start.5 = (bf16[3072,512]{1,0:T(8,128)(2,1)S(1)}, bf16[3072,512]{1,0:T(8,128)(2,1)}, u32[]{:S(2)}) copy-start(bf16[3072,512]{1,0:T(8,128)(2,1)} %copy-done.4) | copy-start | bytes 9437188
  237.9 70.6 %copy-start.11 = (bf16[3072,1376]{0,1:T(8,128)(2,1)S(1)}, bf16[3072,1376]{0,1:T(8,128)(2,1)}, u32[]{:S(2)}) copy-start(bf16[3072,1376]{0,1:T(8,128)(2,1)} %all-gather.5.cloned.1.call-done) | copy-start | bytes 25362436
  255.0 53.5 %copy-start.3 = (bf16[3072,512]{1,0:T(8,128)(2,1)S(1)}, bf16[3072,512]{1,0:T(8,128)(2,1)}, u32[]{:S(2)}) copy-start(bf16[3072,512]{1,0:T(8,128)(2,1)} %copy-done.2) | copy-start | bytes 9437188
  306.2 55.9 %copy-start.7 = (bf16[768,512]{1,0:T(8,128)(2,1)S(1)}, bf16[768,512]{1,0:T(8,128)(2,1)}, u32[]{:S(2)}) copy-start(bf16[768,512]{1,0:T(8,128)(2,1)} %param.16) | copy-start | bytes 2359300
  306.2 55.9 %collective-permute-start.7 = (bf16[768,512]{1,0:T(8,128)(2,1)S(1)}, bf16[768,512]{1,0:T(8,128)(2,1)S(1)}, u32[]{:S(2)}, u32[]{:S(2)}) collective-permute-start(bf16[768,512]{1,0:T(8,128)(2,1)S(1)} %fusion.28), channel_id=1, source_target_pairs={{0,0},{1,1},{2,8},{3,9},{4,16},{5,17},{6,24},{7,25},{8,2},{9,3},{1... | collective-permute-start | bytes 2359304 | tf_op jit(solution)/shard_map/ppermute | solution.py:132
  362.1 6.6 %copy-start.1 = (bf16[1024,1376]{0,1:T(8,128)(2,1)S(1)}, bf16[1024,1376]{0,1:T(8,128)(2,1)}, u32[]{:S(2)}) copy-start(bf16[1024,1376]{0,1:T(8,128)(2,1)} %param.26) | copy-start | bytes 8454148
Sparse Core Ops, SparseCore 0:
  12.4 121.2 all-gather.2
  136.1 88.6 all-gather.4
  227.9 104.2 reduce-scatter.1
